TPU v7x, 32 devices: a whole 2x2x4 slice. The times are simulated.
32 devices in a mesh: tile: 16 (over z, y, x), lev: 2 (over core).
Axes of the slice: x: 2, y: 2, z: 4, core: 2. Of those that a mesh axis runs over, the one named last changes fastest.
Arguments:
- increments: bfloat16 [136, 256, 1024], P('lev', 'tile'), may hold values from -30 to 30
- projection: bfloat16 [80, 136], replicated, may hold values from -0.5 to 0.5
- helmholtz: float32 [80], P('lev'), may hold values from 0.05 to 4
Outputs:
- solution: float32 [80, 256, 1024], P('lev', 'tile')
- residual: float32 [80, 256, 1024], P('lev', 'tile')
All inputs are finite; a program needn't handle non-finite values.
Results may differ from a plain program's by a relative error of at most 0.00075.
Values may be sent and summed in bfloat16 or wider, within the bound.
A program may use at most 192 MiB of HBM per device.

v0:
```python
import jax
import jax.numpy as jnp
import numpy as np
from jax import lax
from jax.sharding import PartitionSpec as P

S = 4
BLOCKS = 2
highest = lax.Precision.HIGHEST


def extended(block, sides, width):
    for axis, dim in sides:
        count = lax.axis_size(axis)
        forward = [(i, i + 1) for i in range(count - 1)]
        backward = [(target, source) for source, target in forward]
        low = lax.ppermute(
            lax.slice_in_dim(block, block.shape[dim] - width, None, axis=dim), axis, forward
        )
        high = lax.ppermute(lax.slice_in_dim(block, 0, width, axis=dim), axis, backward)
        block = jnp.concatenate([low, block, high], axis=dim)
    return block


def shift_matrix():
    width = 2 * S + 1
    table = np.zeros((width, width), np.float32)
    for index in range(S):
        table[index + 1, index] = 1.0
    for index in range(S - 1):
        table[S + 2 + index, S + 1 + index] = 1.0
    return jnp.asarray(table, jnp.float32)


def stencil_rows(field, weight_col):
    padded = extended(field, (("tile", 1),), 1)
    side = jnp.pad(field, ((0, 0), (0, 0), (1, 1)))
    beside_all = padded[:, 2:, :] + padded[:, :-2, :] + side[:, :, 2:] + side[:, :, :-2]
    return weight_col * beside_all


def quadratic(gram, left, right):
    return jnp.einsum("ma,mab,mb->m", left, gram, right, precision=highest)


def combine(coef, vectors):
    total = coef[:, 0, None, None] * vectors[0]
    for index in range(1, len(vectors)):
        total = total + coef[:, index, None, None] * vectors[index]
    return total


def inner_table(vectors):
    width = len(vectors)
    cached = {}
    for first in range(width):
        for second in range(first, width):
            cached[first, second] = jnp.sum(vectors[first] * vectors[second], axis=(1, 2))
    rows_list = []
    for first in range(width):
        entries = []
        for second in range(width):
            entries.append(cached[min(first, second), max(first, second)])
        rows_list.append(jnp.stack(entries, axis=1))
    return jnp.stack(rows_list, axis=1)


def shards(increments, projection, helmholtz):
    lev_count, rows_x, cells_y = increments.shape
    mode_count = projection.shape[0] // lax.axis_size("lev")
    flat = increments.reshape(lev_count, rows_x * cells_y)
    own_cols = lax.dynamic_slice_in_dim(projection, lax.axis_index("lev") * lev_count, lev_count, 1)
    modal = lax.psum_scatter(
        jnp.dot(own_cols, flat, preferred_element_type=jnp.float32),
        "lev",
        scatter_dimension=0,
        tiled=True,
    )
    modal = modal.reshape(mode_count, rows_x, cells_y)
    weight_col = (1.0 / (4.0 + helmholtz))[:, None, None]
    width = 2 * S + 1
    shifter = shift_matrix()
    solution = jnp.zeros_like(modal)
    resid = modal
    direction = modal
    for block_index in range(BLOCKS):
        vectors = [direction]
        current = direction
        for power_index in range(S):
            current = stencil_rows(current, weight_col)
            vectors.append(current)
        vectors.append(resid)
        current = resid
        for power_index in range(S - 1):
            current = stencil_rows(current, weight_col)
            vectors.append(current)
        gram = inner_table(vectors)
        gram = lax.psum(gram, "tile")
        p_coef = jnp.zeros((mode_count, width), jnp.float32).at[:, 0].set(1.0)
        r_coef = jnp.zeros((mode_count, width), jnp.float32).at[:, S + 1].set(1.0)
        x_coef = jnp.zeros((mode_count, width), jnp.float32)
        squares = quadratic(gram, r_coef, r_coef)
        for step_index in range(S):
            moved = p_coef - jnp.einsum("ab,mb->ma", shifter, p_coef, precision=highest)
            alpha = (squares / quadratic(gram, p_coef, moved))[:, None]
            x_coef = x_coef + alpha * p_coef
            r_coef = r_coef - alpha * moved
            fresh = quadratic(gram, r_coef, r_coef)
            p_coef = r_coef + (fresh / squares)[:, None] * p_coef
            squares = fresh
        solution = solution + combine(x_coef, vectors)
        resid = combine(r_coef, vectors)
        direction = combine(p_coef, vectors)
    return (solution, resid)


def solution(mesh):
    in_specs = (P("lev", "tile", None), P(), P("lev"))
    out_specs = (P("lev", "tile", None), P("lev", "tile", None))
    return jax.shard_map(shards, mesh=mesh, in_specs=in_specs, out_specs=out_specs, check_vma=False)
```

profile of v0, /device:TPU:0, one launch (start us, length us, event | category | flops | bytes accessed | tf_op | source)
XLA Modules:
  0.0 469.2 jit_solution(7739262353369601456)
XLA Ops:
  7.2 2.0 pad.144
  9.2 2.9 copy.235
  12.1 4.9 %fusion.44 = f32[80,16384]{1,0:T(8,128)} fusion(bf16[68,16384]{1,0:T(8,128)(2,1)} %bitcast.230, bf16[80,136]{0,1:T(8,128)(2,1)S(1)} %copy-done, s32[]{:T(128)S(6)} %select_n.3), kind=kOutput, calls=%fused_computation.212 | convolution fusion | flops 178257920 | bytes 7489540 | tf_op jit(solution)/shard_map/dot_general | solution.py:74
  17.0 15.9 %reduce-scatter.2.cloned.1.call-done = f32[40,16384]{1,0:T(8,128)} async-done(((f32[80,16384]{1,0:T(8,128)}), f32[40,16384]{1,0:T(8,128)}) %reduce-scatter.2.cloned.1.call-update) | async-done | bytes 2621456 | tf_op jit(solution)/shard_map/reduce_scatter | solution.py:73
  32.9 2.0 copy.251
  36.3 4.6 collective-permute-start.1
  40.9 2.4 collective-permute-done
  43.3 4.5 collective-permute-done.1
  47.8 1.4 fusion.2
  52.1 5.0 %collective-permute-start.3 = (f32[40,1,1024]{2,0,1:T(8,128)S(1)}, f32[40,1,1024]{2,0,1:T(8,128)S(1)}, u32[]{:S(2)}, u32[]{:S(2)}) collective-permute-start(f32[40,1,1024]{2,0,1:T(8,128)S(1)} %get-tuple-element.129), channel_id=1, source_target_pairs={{0,2},{2,4},{4,6},{6,8},{8,10},{10,12},{12,14},{14,16},{16,18},{18... | collective-permute-start | bytes 491528 | tf_op jit(solution)/shard_map/ppermute | solution.py:17
  59.9 1.9 collective-permute-done.3
  61.8 5.6 %fusion.5 = f32[40,16,1024]{2,0,1:T(8,128)S(1)} fusion(f32[40,16,1024]{2,0,1:T(8,128)} %copy-done.18, f32[40,1,1024]{2,0,1:T(8,128)S(1)} %collective-permute-done.3, f32[40,1,1024]{2,0,1:T(8,128)S(1)} %collective-permute-done.2, f32[40]{0:T(128)S(1)} %add_divide_fusion), kind=kLoop, calls=%fused_computation.27 | loop fusion | flops 3932160 | bytes 5570720 | tf_op jit(solution)/shard_map/mul | solution.py:39
  69.6 5.0 %collective-permute-start.5 = (f32[40,1,1024]{2,0,1:T(8,128)}, f32[40,1,1024]{2,0,1:T(8,128)S(1)}, u32[]{:S(2)}, u32[]{:S(2)}) collective-permute-start(f32[40,1,1024]{2,0,1:T(8,128)} %get-tuple-element.127), channel_id=1, source_target_pairs={{0,2},{2,4},{4,6},{6,8},{8,10},{10,12},{12,14},{14,16},{16,18},{18... | collective-permute-start | bytes 491528 | tf_op jit(solution)/shard_map/ppermute | solution.py:17
  75.0 2.3 collective-permute-done.4
  77.3 4.5 collective-permute-done.5
  81.8 5.5 %fusion.8 = f32[40,16,1024]{2,0,1:T(8,128)S(1)} fusion(f32[40,16,1024]{2,0,1:T(8,128)} %copy-done.6, f32[40,1,1024]{2,0,1:T(8,128)S(1)} %collective-permute-done.5, f32[40,1,1024]{2,0,1:T(8,128)S(1)} %collective-permute-done.4, f32[40]{0:T(128)S(1)} %add_divide_fusion), kind=kLoop, calls=%fused_computation.30 | loop fusion | flops 3932160 | bytes 5570720 | tf_op jit(solution)/shard_map/mul | solution.py:39
  87.4 1.6 collective-permute-start.6
  88.9 4.9 %collective-permute-start.7 = (f32[40,1,1024]{2,0,1:T(8,128)S(1)}, f32[40,1,1024]{2,0,1:T(8,128)S(1)}, u32[]{:S(2)}, u32[]{:S(2)}) collective-permute-start(f32[40,1,1024]{2,0,1:T(8,128)S(1)} %get-tuple-element.125), channel_id=1, source_target_pairs={{0,2},{2,4},{4,6},{6,8},{8,10},{10,12},{12,14},{14,16},{16,18},{18... | collective-permute-start | bytes 491528 | tf_op jit(solution)/shard_map/ppermute | solution.py:17
  94.1 2.2 collective-permute-done.6
  96.3 2.2 collective-permute-done.7
  98.5 5.4 %multiply_reduce_fusion.45 = (f32[40]{0:T(128)S(1)}, f32[40]{0:T(128)S(1)}, f32[40]{0:T(128)S(1)}, f32[40]{0:T(128)S(1)}, f32[40]{0:T(128)S(1)}, /*index=5*/f32[...) fusion(f32[40,16,1024]{2,0,1:T(8,128)S(1)} %fusion.8, ...), kind=kLoop, calls=%fused_computation.138 | loop fusion | flops 26213840 | bytes 11143520 | tf_op jit(solution)/shard_map/reduce_sum | solution.py:58
  104.2 75.3 %psum.14 = f32[40,9,9]{0,2,1:T(8,128)S(1)} all-reduce(f32[40,9,9]{0,2,1:T(8,128)S(1)} %constant_dynamic-update-slice_fusion), channel_id=1, replica_groups=mesh['tile'=16,'lev'=2] {'tile'}, use_global_device_ids=true, to_apply=%region_17.18 | all-reduce | flops 3240 | bytes 25920 | tf_op jit(solution)/shard_map/psum | solution.py:98
  183.8 13.6 %multiply_add_fusion.2 = f32[40,16,1024]{2,0,1:T(8,128)S(1)} fusion(f32[40,16,1024]{2,0,1:T(8,128)} %copy-done.6, f32[40,16,1024]{2,0,1:T(8,128)} %get-tuple-element.109, f32[40]{0:T(128)S(1)} %get-tuple-element.162, f32[40]{0:T(128)S(1)} %get-tuple-element.163, f32[40]{0:T(128)S(1)} %get-tuple-element.164, f32[40]{0:T(128)S(1)} %get-tuple-element.165, ...), kind=kLoop, calls=%fused_computation.137 | loop fusion | flops 19005440 | bytes 13764160 | tf_op jit(solution)/shard_map/add | solution.py:49
  198.7 4.6 collective-permute-start.9
  203.3 5.8 %multiply_add_fusion.1 = f32[40,16,1024]{2,0,1:T(8,128)S(1)} fusion(f32[40,16,1024]{2,0,1:T(8,128)S(1)} %copy-done.7, f32[40,16,1024]{2,0,1:T(8,128)S(1)} %copy-done.17, f32[40]{0:T(128)S(1)} %get-tuple-element.171, f32[40]{0:T(128)S(1)} %get-tuple-element.172, f32[40]{0:T(128)S(1)} %get-tuple-element.173, f32[40]{0:T(128)S(1)} %get-tuple-element.174, ...), kind=kLoop, calls=%fused_computation.131 | loop fusion | flops 19005440 | bytes 13764160 | tf_op jit(solution)/shard_map/add | solution.py:49
  209.2 1.4 fusion.14
  211.9 4.6 collective-permute-start.11
  217.8 4.6 collective-permute-start.17
  222.4 1.4 fusion.17
  225.2 5.0 %collective-permute-start.13 = (f32[40,1,1024]{2,0,1:T(8,128)S(1)}, f32[40,1,1024]{2,0,1:T(8,128)S(1)}, u32[]{:S(2)}, u32[]{:S(2)}) collective-permute-start(f32[40,1,1024]{2,0,1:T(8,128)S(1)} %get-tuple-element.115), channel_id=1, source_target_pairs={{0,2},{2,4},{4,6},{6,8},{8,10},{10,12},{12,14},{14,16},{16,18},{18... | collective-permute-start | bytes 491528 | tf_op jit(solution)/shard_map/ppermute | solution.py:17
  230.2 2.3 collective-permute-done.12
  232.6 2.0 collective-permute-done.13
  234.5 3.3 fusion.20
  239.2 6.9 %collective-permute-start.19 = (f32[40,1,1024]{2,0,1:T(8,128)S(1)}, f32[40,1,1024]{2,0,1:T(8,128)S(1)}, u32[]{:S(2)}, u32[]{:S(2)}) collective-permute-start(f32[40,1,1024]{2,0,1:T(8,128)S(1)} %get-tuple-element.121), channel_id=1, source_target_pairs={{0,2},{2,4},{4,6},{6,8},{8,10},{10,12},{12,14},{14,16},{16,18},{18... | collective-permute-start | bytes 491528 | tf_op jit(solution)/shard_map/ppermute | solution.py:17
  247.4 6.1 %collective-permute-start.15 = (f32[40,1,1024]{2,0,1:T(8,128)S(1)}, f32[40,1,1024]{2,0,1:T(8,128)}, u32[]{:S(2)}, u32[]{:S(2)}) collective-permute-start(f32[40,1,1024]{2,0,1:T(8,128)S(1)} %get-tuple-element.113), channel_id=1, source_target_pairs={{0,2},{2,4},{4,6},{6,8},{8,10},{10,12},{12,14},{14,16},{16,18},{18... | collective-permute-start | bytes 491528 | tf_op jit(solution)/shard_map/ppermute | solution.py:17
  253.6 1.4 fusion.29
  255.1 1.5 copy-done.20
  257.8 5.7 %collective-permute-start.21 = (f32[40,1,1024]{2,0,1:T(8,128)S(1)}, f32[40,1,1024]{2,0,1:T(8,128)}, u32[]{:S(2)}, u32[]{:S(2)}) collective-permute-start(f32[40,1,1024]{2,0,1:T(8,128)S(1)} %get-tuple-element.111), channel_id=1, source_target_pairs={{0,2},{2,4},{4,6},{6,8},{8,10},{10,12},{12,14},{14,16},{16,18},{18... | collective-permute-start | bytes 491528 | tf_op jit(solution)/shard_map/ppermute | solution.py:17
  264.3 1.4 collective-permute-done.21
  265.7 24.5 %multiply_reduce_fusion = (f32[40]{0:T(128)}, f32[40]{0:T(128)}, f32[40]{0:T(128)}, f32[40]{0:T(128)}, f32[40]{0:T(128)}, /*index=5*/f32[40]{0:T(128)}, f32[40]{...) fusion(f32[40,16,1024]{2,0,1:T(8,128)} %copy-done.20, ...), kind=kLoop, calls=%fused_computation.91 | loop fusion | flops 70777080 | bytes 21961920 | tf_op jit(solution)/shard_map/reduce_sum | solution.py:58
  295.9 1.4 stack.449
  297.3 1.4 stack.442
  301.4 1.4 stack.415
  308.2 77.3 %psum.15 = f32[40,9,9]{0,2,1:T(8,128)S(1)} all-reduce(f32[40,9,9]{0,2,1:T(8,128)} %constant_dynamic-update-slice_fusion.9), channel_id=1, replica_groups=mesh['tile'=16,'lev'=2] {'tile'}, use_global_device_ids=true, to_apply=%region_64.65 | all-reduce | flops 3240 | bytes 25920 | tf_op jit(solution)/shard_map/psum | solution.py:98
  422.2 19.2 %multiply_add_fusion = f32[40,16,1024]{2,0,1:T(8,128)} fusion(f32[40,16,1024]{2,0,1:T(8,128)} %get-tuple-element.108, f32[40,16,1024]{2,0,1:T(8,128)} %copy-done.15, f32[40,16,1024]{2,0,1:T(8,128)} %copy-done.11, f32[40,16,1024]{2,0,1:T(8,128)} %get-tuple-element.107, f32[40,16,1024]{2,0,1:T(8,128)} %copy-done.16, f32[40,16,1024]{2,0,1:T(8,128)} %copy-done.13, ...), kind=kLoop, calls=%fused_computation.89 | loop fusion | flops 19005440 | bytes 21628480 | tf_op jit(solution)/shard_map/add | solution.py:49
  441.5 4.9 %copy.22 = f32[40,16,1024]{2,1,0:T(8,128)} copy(f32[40,16,1024]{2,0,1:T(8,128)} %multiply_add_fusion) | data formatting | bytes 5242880
  446.5 12.8 %add_add_fusion = f32[40,16,1024]{2,0,1:T(8,128)S(1)} fusion(f32[40,16,1024]{2,0,1:T(8,128)} %get-tuple-element.108, f32[40,16,1024]{2,0,1:T(8,128)} %copy-done.15, f32[40,16,1024]{2,0,1:T(8,128)S(1)} %copy-done.12, f32[40,16,1024]{2,0,1:T(8,128)} %get-tuple-element.107, f32[40,16,1024]{2,0,1:T(8,128)} %copy-done.16, f32[40,16,1024]{2,0,1:T(8,128)S(1)} %copy-done.14, ...), kind=kLoop, calls=%fused_computation.90 | loop fusion | flops 38666240 | bytes 32771040 | tf_op jit(solution)/shard_map/add | solution.py:111
  459.3 3.0 copy.21
  (319 shorter events, 73.1 us)
Async XLA Ops:
  7.2 25.7 %reduce-scatter.2.cloned.1.call-start = ((), (), s32[]{:S(2)}) async-start(), calls=%async_computation.1 | async-start | bytes 7864320 | tf_op jit(solution)/shard_map/reduce_scatter | solution.py:73
  34.9 14.3 %copy-start.3 = (f32[5,16,8,1024]{3,2,0,1:T(8,128)}, f32[5,16,8,1024]{3,2,0,1:T(8,128)S(1)}, u32[]{:S(2)}) copy-start(f32[5,16,8,1024]{3,2,0,1:T(8,128)S(1)} %copy.251) | copy-start | bytes 7864324
  35.0 8.3 %collective-permute-start = (f32[40,1,1024]{2,0,1:T(8,128)S(1)}, f32[40,1,1024]{2,0,1:T(8,128)S(1)}, u32[]{:S(2)}, u32[]{:S(2)}) collective-permute-start(f32[40,1,1024]{2,0,1:T(8,128)S(1)} %get-tuple-element.130), channel_id=1, source_target_pairs={{2,0},{4,2},{6,4},{8,6},{10,8},{12,10},{14,12},{16,14},{18,16},{20... | collective-permute-start | bytes 491528 | tf_op jit(solution)/shard_map/ppermute | solution.py:20
  36.3 11.5 %collective-permute-start.1 = (f32[40,1,1024]{2,0,1:T(8,128)S(1)}, f32[40,1,1024]{2,0,1:T(8,128)S(1)}, u32[]{:S(2)}, u32[]{:S(2)}) collective-permute-start(f32[40,1,1024]{2,0,1:T(8,128)S(1)} %get-tuple-element.131), channel_id=1, source_target_pairs={{0,2},{2,4},{4,6},{6,8},{8,10},{10,12},{12,14},{14,16},{16,18},{18... | collective-permute-start | bytes 491528 | tf_op jit(solution)/shard_map/ppermute | solution.py:17
  40.9 142.9 %copy-start.35 = (f32[40]{0:T(128)}, f32[40]{0:T(128)S(1)}, u32[]{:S(2)}) copy-start(f32[40]{0:T(128)S(1)} %add_divide_fusion) | copy-start | bytes 484
  50.8 9.1 %collective-permute-start.2 = (f32[40,1,1024]{2,0,1:T(8,128)}, f32[40,1,1024]{2,0,1:T(8,128)S(1)}, u32[]{:S(2)}, u32[]{:S(2)}) collective-permute-start(f32[40,1,1024]{2,0,1:T(8,128)} %get-tuple-element.128), channel_id=1, source_target_pairs={{2,0},{4,2},{6,4},{8,6},{10,8},{12,10},{14,12},{16,14},{18,16},{20... | collective-permute-start | bytes 491528 | tf_op jit(solution)/shard_map/ppermute | solution.py:20
  52.1 9.7 %collective-permute-start.3 = (f32[40,1,1024]{2,0,1:T(8,128)S(1)}, f32[40,1,1024]{2,0,1:T(8,128)S(1)}, u32[]{:S(2)}, u32[]{:S(2)}) collective-permute-start(f32[40,1,1024]{2,0,1:T(8,128)S(1)} %get-tuple-element.129), channel_id=1, source_target_pairs={{0,2},{2,4},{4,6},{6,8},{8,10},{10,12},{12,14},{14,16},{16,18},{18... | collective-permute-start | bytes 491528 | tf_op jit(solution)/shard_map/ppermute | solution.py:17
  59.9 121.4 %copy-start.39 = (f32[9]{0:T(128)}, f32[9]{0:T(128)S(1)}, u32[]{:S(2)}) copy-start(f32[9]{0:T(128)S(1)} %scatter.16) | copy-start | bytes 112
  59.9 14.8 %copy-start.30 = (f32[9,9]{1,0:T(8,128)S(1)}, f32[9,9]{1,0:T(8,128)}, u32[]{:S(2)}) copy-start(f32[9,9]{1,0:T(8,128)} %constant.100.clone) | copy-start | bytes 976
  68.3 9.0 %collective-permute-start.4 = (f32[40,1,1024]{2,0,1:T(8,128)}, f32[40,1,1024]{2,0,1:T(8,128)S(1)}, u32[]{:S(2)}, u32[]{:S(2)}) collective-permute-start(f32[40,1,1024]{2,0,1:T(8,128)} %get-tuple-element.126), channel_id=1, source_target_pairs={{2,0},{4,2},{6,4},{8,6},{10,8},{12,10},{14,12},{16,14},{18,16},{20... | collective-permute-start | bytes 491528 | tf_op jit(solution)/shard_map/ppermute | solution.py:20
  69.6 12.2 %collective-permute-start.5 = (f32[40,1,1024]{2,0,1:T(8,128)}, f32[40,1,1024]{2,0,1:T(8,128)S(1)}, u32[]{:S(2)}, u32[]{:S(2)}) collective-permute-start(f32[40,1,1024]{2,0,1:T(8,128)} %get-tuple-element.127), channel_id=1, source_target_pairs={{0,2},{2,4},{4,6},{6,8},{8,10},{10,12},{12,14},{14,16},{16,18},{18... | collective-permute-start | bytes 491528 | tf_op jit(solution)/shard_map/ppermute | solution.py:17
  74.9 108.1 %copy-start.24 = (f32[40,9]{0,1:T(8,128)}, f32[40,9]{0,1:T(8,128)S(1)}, u32[]{:S(2)}) copy-start(f32[40,9]{0,1:T(8,128)S(1)} %convolution_subtract_fusion.6) | copy-start | bytes 4324
  75.0 104.8 %copy-start.33 = (f32[40,9]{1,0:T(8,128)}, f32[40,9]{1,0:T(8,128)S(1)}, u32[]{:S(2)}) copy-start(f32[40,9]{1,0:T(8,128)S(1)} %copy.40) | copy-start | bytes 4324
  75.0 18.9 %copy-start.2 = (f32[40,16384]{1,0:T(8,128)S(1)}, f32[40,16384]{1,0:T(8,128)}, u32[]{:S(2)}) copy-start(f32[40,16384]{1,0:T(8,128)} %reduce-scatter.2.cloned.1.call-done) | copy-start | bytes 7864324
  81.8 121.4 %copy-start.21 = (f32[40,1,1024]{2,0,1:T(8,128)}, f32[40,1,1024]{2,0,1:T(8,128)S(1)}, u32[]{:S(2)}) copy-start(f32[40,1,1024]{2,0,1:T(8,128)S(1)} %collective-permute-done.5) | copy-start | bytes 491524
  87.3 11.2 %copy-start.19 = (f32[40,16,1024]{2,0,1:T(8,128)S(1)}, f32[40,16,1024]{2,0,1:T(8,128)}, u32[]{:S(2)}) copy-start(f32[40,16,1024]{2,0,1:T(8,128)} %copy-done.18) | copy-start | bytes 7864324
  87.3 11.2 %copy-start.27 = (f32[40,1,1024]{2,0,1:T(8,128)S(1)}, f32[40,1,1024]{2,0,1:T(8,128)}, u32[]{:S(2)}) copy-start(f32[40,1,1024]{2,0,1:T(8,128)} %copy-done.26) | copy-start | bytes 491524
  87.4 8.9 %collective-permute-start.6 = (f32[40,1,1024]{2,0,1:T(8,128)S(1)}, f32[40,1,1024]{2,0,1:T(8,128)S(1)}, u32[]{:S(2)}, u32[]{:S(2)}) collective-permute-start(f32[40,1,1024]{2,0,1:T(8,128)S(1)} %get-tuple-element.124), channel_id=1, source_target_pairs={{2,0},{4,2},{6,4},{8,6},{10,8},{12,10},{14,12},{16,14},{18,16},{20... | collective-permute-start | bytes 491528 | tf_op jit(solution)/shard_map/ppermute | solution.py:20
  88.9 9.6 %collective-permute-start.7 = (f32[40,1,1024]{2,0,1:T(8,128)S(1)}, f32[40,1,1024]{2,0,1:T(8,128)S(1)}, u32[]{:S(2)}, u32[]{:S(2)}) collective-permute-start(f32[40,1,1024]{2,0,1:T(8,128)S(1)} %get-tuple-element.125), channel_id=1, source_target_pairs={{0,2},{2,4},{4,6},{6,8},{8,10},{10,12},{12,14},{14,16},{16,18},{18... | collective-permute-start | bytes 491528 | tf_op jit(solution)/shard_map/ppermute | solution.py:17
  183.8 19.5 %copy-start.4 = (f32[5,16,8,1024]{3,2,0,1:T(8,128)S(1)}, f32[5,16,8,1024]{3,2,0,1:T(8,128)}, u32[]{:S(2)}) copy-start(f32[5,16,8,1024]{3,2,0,1:T(8,128)} %copy-done.3) | copy-start | bytes 7864324
  183.8 19.5 %copy-start.7 = (f32[40,16,1024]{2,0,1:T(8,128)S(1)}, f32[40,16,1024]{2,0,1:T(8,128)}, u32[]{:S(2)}) copy-start(f32[40,16,1024]{2,0,1:T(8,128)} %copy-done.6) | copy-start | bytes 7864324
  183.8 19.5 %copy-start.17 = (f32[40,16,1024]{2,0,1:T(8,128)S(1)}, f32[40,16,1024]{2,0,1:T(8,128)}, u32[]{:S(2)}) copy-start(f32[40,16,1024]{2,0,1:T(8,128)} %get-tuple-element.109) | copy-start | bytes 7864324
  197.4 68.4 %copy-start.9 = (f32[40,16,1024]{2,0,1:T(8,128)}, f32[40,16,1024]{2,0,1:T(8,128)S(1)}, u32[]{:S(2)}) copy-start(f32[40,16,1024]{2,0,1:T(8,128)S(1)} %multiply_add_fusion.2) | copy-start | bytes 7864324
  197.4 11.7 %collective-permute-start.8 = (f32[40,1,1024]{2,0,1:T(8,128)S(1)}, f32[40,1,1024]{2,0,1:T(8,128)S(1)}, u32[]{:S(2)}, u32[]{:S(2)}) collective-permute-start(f32[40,1,1024]{2,0,1:T(8,128)S(1)} %get-tuple-element.118), channel_id=1, source_target_pairs={{2,0},{4,2},{6,4},{8,6},{10,8},{12,10},{14,12},{16,14},{18,16},{20... | collective-permute-start | bytes 491528 | tf_op jit(solution)/shard_map/ppermute | solution.py:20
  198.7 10.4 %collective-permute-start.9 = (f32[40,1,1024]{2,0,1:T(8,128)S(1)}, f32[40,1,1024]{2,0,1:T(8,128)S(1)}, u32[]{:S(2)}, u32[]{:S(2)}) collective-permute-start(f32[40,1,1024]{2,0,1:T(8,128)S(1)} %get-tuple-element.119), channel_id=1, source_target_pairs={{0,2},{2,4},{4,6},{6,8},{8,10},{10,12},{12,14},{14,16},{16,18},{18... | collective-permute-start | bytes 491528 | tf_op jit(solution)/shard_map/ppermute | solution.py:17
  209.1 56.6 %copy-start.11 = (f32[40,16,1024]{2,0,1:T(8,128)}, f32[40,16,1024]{2,0,1:T(8,128)S(1)}, u32[]{:S(2)}) copy-start(f32[40,16,1024]{2,0,1:T(8,128)S(1)} %multiply_add_fusion.1) | copy-start | bytes 7864324
  210.6 55.1 %copy-start.13 = (f32[40,16,1024]{2,0,1:T(8,128)}, f32[40,16,1024]{2,0,1:T(8,128)S(1)}, u32[]{:S(2)}) copy-start(f32[40,16,1024]{2,0,1:T(8,128)S(1)} %fusion.14) | copy-start | bytes 7864324
  210.6 11.8 %collective-permute-start.10 = (f32[40,1,1024]{2,0,1:T(8,128)S(1)}, f32[40,1,1024]{2,0,1:T(8,128)S(1)}, u32[]{:S(2)}, u32[]{:S(2)}) collective-permute-start(f32[40,1,1024]{2,0,1:T(8,128)S(1)} %get-tuple-element.116), channel_id=1, source_target_pairs={{2,0},{4,2},{6,4},{8,6},{10,8},{12,10},{14,12},{16,14},{18,16},{20... | collective-permute-start | bytes 491528 | tf_op jit(solution)/shard_map/ppermute | solution.py:20
  211.9 10.5 %collective-permute-start.11 = (f32[40,1,1024]{2,0,1:T(8,128)S(1)}, f32[40,1,1024]{2,0,1:T(8,128)S(1)}, u32[]{:S(2)}, u32[]{:S(2)}) collective-permute-start(f32[40,1,1024]{2,0,1:T(8,128)S(1)} %get-tuple-element.117), channel_id=1, source_target_pairs={{0,2},{2,4},{4,6},{6,8},{8,10},{10,12},{12,14},{14,16},{16,18},{18... | collective-permute-start | bytes 491528 | tf_op jit(solution)/shard_map/ppermute | solution.py:17
  216.5 13.7 %collective-permute-start.16 = (f32[40,1,1024]{2,0,1:T(8,128)S(1)}, f32[40,1,1024]{2,0,1:T(8,128)S(1)}, u32[]{:S(2)}, u32[]{:S(2)}) collective-permute-start(f32[40,1,1024]{2,0,1:T(8,128)S(1)} %get-tuple-element.122), channel_id=1, source_target_pairs={{2,0},{4,2},{6,4},{8,6},{10,8},{12,10},{14,12},{16,14},{18,16},{20... | collective-permute-start | bytes 491528 | tf_op jit(solution)/shard_map/ppermute | solution.py:20
  217.8 12.4 %collective-permute-start.17 = (f32[40,1,1024]{2,0,1:T(8,128)S(1)}, f32[40,1,1024]{2,0,1:T(8,128)S(1)}, u32[]{:S(2)}, u32[]{:S(2)}) collective-permute-start(f32[40,1,1024]{2,0,1:T(8,128)S(1)} %get-tuple-element.123), channel_id=1, source_target_pairs={{0,2},{2,4},{4,6},{6,8},{8,10},{10,12},{12,14},{14,16},{16,18},{18... | collective-permute-start | bytes 491528 | tf_op jit(solution)/shard_map/ppermute | solution.py:17
  223.9 8.7 %collective-permute-start.12 = (f32[40,1,1024]{2,0,1:T(8,128)S(1)}, f32[40,1,1024]{2,0,1:T(8,128)S(1)}, u32[]{:S(2)}, u32[]{:S(2)}) collective-permute-start(f32[40,1,1024]{2,0,1:T(8,128)S(1)} %get-tuple-element.114), channel_id=1, source_target_pairs={{2,0},{4,2},{6,4},{8,6},{10,8},{12,10},{14,12},{16,14},{18,16},{20... | collective-permute-start | bytes 491528 | tf_op jit(solution)/shard_map/ppermute | solution.py:20
  225.2 9.3 %collective-permute-start.13 = (f32[40,1,1024]{2,0,1:T(8,128)S(1)}, f32[40,1,1024]{2,0,1:T(8,128)S(1)}, u32[]{:S(2)}, u32[]{:S(2)}) collective-permute-start(f32[40,1,1024]{2,0,1:T(8,128)S(1)} %get-tuple-element.115), channel_id=1, source_target_pairs={{0,2},{2,4},{4,6},{6,8},{8,10},{10,12},{12,14},{14,16},{16,18},{18... | collective-permute-start | bytes 491528 | tf_op jit(solution)/shard_map/ppermute | solution.py:17
  237.8 17.2 %copy-start.15 = (f32[40,16,1024]{2,0,1:T(8,128)}, f32[40,16,1024]{2,0,1:T(8,128)S(1)}, u32[]{:S(2)}) copy-start(f32[40,16,1024]{2,0,1:T(8,128)S(1)} %get-tuple-element.182) | copy-start | bytes 7864324
  237.9 17.2 %copy-start.16 = (f32[40,16,1024]{2,0,1:T(8,128)}, f32[40,16,1024]{2,0,1:T(8,128)S(1)}, u32[]{:S(2)}) copy-start(f32[40,16,1024]{2,0,1:T(8,128)S(1)} %get-tuple-element.181) | copy-start | bytes 7864324
  237.9 15.7 %collective-permute-start.18 = (f32[40,1,1024]{2,0,1:T(8,128)S(1)}, f32[40,1,1024]{2,0,1:T(8,128)S(1)}, u32[]{:S(2)}, u32[]{:S(2)}) collective-permute-start(f32[40,1,1024]{2,0,1:T(8,128)S(1)} %get-tuple-element.120), channel_id=1, source_target_pairs={{2,0},{4,2},{6,4},{8,6},{10,8},{12,10},{14,12},{16,14},{18,16},{20... | collective-permute-start | bytes 491528 | tf_op jit(solution)/shard_map/ppermute | solution.py:20
  239.2 14.4 %collective-permute-start.19 = (f32[40,1,1024]{2,0,1:T(8,128)S(1)}, f32[40,1,1024]{2,0,1:T(8,128)S(1)}, u32[]{:S(2)}, u32[]{:S(2)}) collective-permute-start(f32[40,1,1024]{2,0,1:T(8,128)S(1)} %get-tuple-element.121), channel_id=1, source_target_pairs={{0,2},{2,4},{4,6},{6,8},{8,10},{10,12},{12,14},{14,16},{16,18},{18... | collective-permute-start | bytes 491528 | tf_op jit(solution)/shard_map/ppermute | solution.py:17
  246.1 18.0 %collective-permute-start.14 = (f32[40,1,1024]{2,0,1:T(8,128)S(1)}, f32[40,1,1024]{2,0,1:T(8,128)}, u32[]{:S(2)}, u32[]{:S(2)}) collective-permute-start(f32[40,1,1024]{2,0,1:T(8,128)S(1)} %get-tuple-element.112), channel_id=1, source_target_pairs={{2,0},{4,2},{6,4},{8,6},{10,8},{12,10},{14,12},{16,14},{18,16},{20... | collective-permute-start | bytes 491528 | tf_op jit(solution)/shard_map/ppermute | solution.py:20
  247.4 16.7 %collective-permute-start.15 = (f32[40,1,1024]{2,0,1:T(8,128)S(1)}, f32[40,1,1024]{2,0,1:T(8,128)}, u32[]{:S(2)}, u32[]{:S(2)}) collective-permute-start(f32[40,1,1024]{2,0,1:T(8,128)S(1)} %get-tuple-element.113), channel_id=1, source_target_pairs={{0,2},{2,4},{4,6},{6,8},{8,10},{10,12},{12,14},{14,16},{16,18},{18... | collective-permute-start | bytes 491528 | tf_op jit(solution)/shard_map/ppermute | solution.py:17
  256.5 7.8 %collective-permute-start.20 = (f32[40,1,1024]{2,0,1:T(8,128)S(1)}, f32[40,1,1024]{2,0,1:T(8,128)}, u32[]{:S(2)}, u32[]{:S(2)}) collective-permute-start(f32[40,1,1024]{2,0,1:T(8,128)S(1)} %get-tuple-element.110), channel_id=1, source_target_pairs={{2,0},{4,2},{6,4},{8,6},{10,8},{12,10},{14,12},{16,14},{18,16},{20... | collective-permute-start | bytes 491528 | tf_op jit(solution)/shard_map/ppermute | solution.py:20
  257.8 7.9 %collective-permute-start.21 = (f32[40,1,1024]{2,0,1:T(8,128)S(1)}, f32[40,1,1024]{2,0,1:T(8,128)}, u32[]{:S(2)}, u32[]{:S(2)}) collective-permute-start(f32[40,1,1024]{2,0,1:T(8,128)S(1)} %get-tuple-element.111), channel_id=1, source_target_pairs={{0,2},{2,4},{4,6},{6,8},{8,10},{10,12},{12,14},{14,16},{16,18},{18... | collective-permute-start | bytes 491528 | tf_op jit(solution)/shard_map/ppermute | solution.py:17
  264.2 124.1 %copy-start.34 = (f32[40,9]{1,0:T(8,128)S(1)}, f32[40,9]{1,0:T(8,128)}, u32[]{:S(2)}) copy-start(f32[40,9]{1,0:T(8,128)} %copy-done.33) | copy-start | bytes 4324
  264.2 127.0 %copy-start.25 = (f32[40,9]{0,1:T(8,128)S(1)}, f32[40,9]{0,1:T(8,128)}, u32[]{:S(2)}) copy-start(f32[40,9]{0,1:T(8,128)} %copy-done.24) | copy-start | bytes 4324
  264.2 133.2 %copy-start.31 = (f32[9,9]{1,0:T(8,128)S(1)}, f32[9,9]{1,0:T(8,128)}, u32[]{:S(2)}) copy-start(f32[9,9]{1,0:T(8,128)} %constant.100.clone) | copy-start | bytes 976
  422.1 24.2 %copy-start.10 = (f32[40,16,1024]{2,0,1:T(8,128)S(1)}, f32[40,16,1024]{2,0,1:T(8,128)}, u32[]{:S(2)}) copy-start(f32[40,16,1024]{2,0,1:T(8,128)} %copy-done.9) | copy-start | bytes 7864324
  422.2 24.2 %copy-start.12 = (f32[40,16,1024]{2,0,1:T(8,128)S(1)}, f32[40,16,1024]{2,0,1:T(8,128)}, u32[]{:S(2)}) copy-start(f32[40,16,1024]{2,0,1:T(8,128)} %copy-done.11) | copy-start | bytes 7864324
  422.2 24.2 %copy-start.14 = (f32[40,16,1024]{2,0,1:T(8,128)S(1)}, f32[40,16,1024]{2,0,1:T(8,128)}, u32[]{:S(2)}) copy-start(f32[40,16,1024]{2,0,1:T(8,128)} %copy-done.13) | copy-start | bytes 7864324
  446.5 15.8 %copy-start.1 = (bf16[80,136]{0,1:T(8,128)(2,1)S(1)}, bf16[80,136]{0,1:T(8,128)(2,1)}, u32[]{:S(2)}) copy-start(bf16[80,136]{0,1:T(8,128)(2,1)} %param.13) | copy-start | bytes 65284
  (48 other events, 225.6 us)
Sparse Core Ops, SparseCore 0:
  17.1 15.7 reduce-scatter.1
where the time goes:
time: 471 us; the launch traced here: 469 us
  blocking collectives  153 us (32%)
  other arithmetic  124 us (26%)
  starting transfers between devices  71.4 us (15%)
  local copies, waits for them, and re-layouts  55.5 us (12%)
  waiting for transfers between devices  41.9 us (9%)
  between operations  16.7 us (4%)
  matrix products  7.1 us (2%)
    psum x2, blocking collectives, shards(): gram = lax.psum(gram, 'tile')  153 us
    ppermute x11, starting transfers between devices, extended(): lax.ppermute(lax.slice_in_dim(block, block.shape[dim] - width, None, axis...  56.9 us
    add x3, other arithmetic, combine(): total = total + coef[:, index, None, None] * vectors[index]  38.5 us
    reduce_sum x3, other arithmetic, inner_table(): jnp.sum(vectors[first] * vectors[second], axis=(1, 2))  30.2 us
    unnamed x180, local copies, waits for them, and re-layouts  29.2 us
    mul x7, other arithmetic, stencil_rows(): return weight_col * beside_all  20.1 us
    ppermute x11, waiting for transfers between devices, extended(): lax.ppermute(lax.slice_in_dim(block, block.shape[dim] - width, None, axis...  16.6 us
    reduce_scatter x1, waiting for transfers between devices, shards(): lax.psum_scatter(jnp.dot(own_cols, flat, preferred_element_type=jnp.float...  15.9 us
  transfers between devices with their start and end apart: 23, of which 12 were waited for; matrix products, arithmetic and copies ran while one was open for 2% of the time, Pallas kernels for 0%

commit v1 on v0

--- a/solution.py
+++ b/solution.py
@@ -95,7 +95,7 @@
             current = stencil_rows(current, weight_col)
             vectors.append(current)
         gram = inner_table(vectors)
-        gram = lax.psum(gram, "tile")
+        gram = jnp.sum(lax.all_gather(gram, "tile"), axis=0)
         p_coef = jnp.zeros((mode_count, width), jnp.float32).at[:, 0].set(1.0)
         r_coef = jnp.zeros((mode_count, width), jnp.float32).at[:, S + 1].set(1.0)
         x_coef = jnp.zeros((mode_count, width), jnp.float32)

time: 471 us -> 581 us (1.23)
  blocking collectives: 153 us -> 246 us
  other arithmetic: 124 us -> 131 us
  local copies, waits for them, and re-layouts: 55.5 us -> 62 us
    all_gather x0 -> x2, blocking collectives: none -> 246 us  [shards(): gram = jnp.sum(lax.all_gather(gram, 'tile'), axis=0)]
    psum x2 -> x0, blocking collectives: 153 us -> none  [shards(): gram = lax.psum(gram, 'tile')]
    reduce_sum x0 -> x2, other arithmetic: none -> 7.39 us  [shards(): gram = jnp.sum(lax.all_gather(gram, 'tile'), axis=0)]
    unnamed x180 -> x162, local copies, waits for them, and re-layouts: 29.2 us -> 30.2 us
  transfers between devices with their start and end apart: 23 -> 23, of which waited for: 12 -> 15; matrix products, arithmetic and copies ran while one was open for 2% -> 2% of each run, Pallas kernels for 0% -> 0%
where the time goes in v1:
time: 581 us; the launch traced here: 579 us
  blocking collectives  246 us (42%)
  other arithmetic  131 us (23%)
  starting transfers between devices  72.5 us (12%)
  local copies, waits for them, and re-layouts  62 us (11%)
  waiting for transfers between devices  44.1 us (8%)
  between operations  16.4 us (3%)
  matrix products  7.1 us (1%)
    all_gather x2, blocking collectives, shards(): gram = jnp.sum(lax.all_gather(gram, 'tile'), axis=0)  246 us
    ppermute x11, starting transfers between devices, extended(): lax.ppermute(lax.slice_in_dim(block, block.shape[dim] - width, None, axis...  58 us
    add x3, other arithmetic, combine(): total = total + coef[:, index, None, None] * vectors[index]  38.5 us
    unnamed x162, local copies, waits for them, and re-layouts  30.2 us
    reduce_sum x3, other arithmetic, inner_table(): jnp.sum(vectors[first] * vectors[second], axis=(1, 2))  30.1 us
    mul x7, other arithmetic, stencil_rows(): return weight_col * beside_all  20.1 us
    ppermute x11, waiting for transfers between devices, extended(): lax.ppermute(lax.slice_in_dim(block, block.shape[dim] - width, None, axis...  19.6 us
    another operation x14, local copies, waits for them, and re-layouts, inner_table(): rows_list.append(jnp.stack(entries, axis=1))  16.7 us
  transfers between devices with their start and end apart: 23, of which 15 were waited for; matrix products, arithmetic and copies ran while one was open for 2% of the time, Pallas kernels for 0%

profile of v1, /device:TPU:0, one launch (start us, length us, event | category | flops | bytes accessed | tf_op | source)
XLA Modules:
  0.0 578.8 jit_solution(1811130278773603440)
XLA Ops:
  7.2 2.0 pad.144
  9.2 2.9 copy.241
  12.1 4.9 fusion.44
  17.0 15.9 %reduce-scatter.2.cloned.1.call-done = f32[40,16384]{1,0:T(8,128)} async-done(((f32[80,16384]{1,0:T(8,128)}), f32[40,16384]{1,0:T(8,128)}) %reduce-scatter.2.cloned.1.call-update) | async-done | bytes 2621456 | tf_op jit(solution)/shard_map/reduce_scatter | solution.py:73
  32.9 2.0 copy.257
  36.3 4.6 collective-permute-start.1
  40.9 2.4 collective-permute-done
  43.3 4.5 collective-permute-done.1
  47.8 1.4 fusion.2
  52.1 5.0 collective-permute-start.3
  59.8 2.0 collective-permute-done.3
  61.8 5.5 fusion.5
  69.5 5.0 collective-permute-start.5
  74.8 2.3 collective-permute-done.4
  77.1 4.5 collective-permute-done.5
  81.7 5.6 fusion.8
  87.4 1.6 collective-permute-start.6
  88.9 4.9 collective-permute-start.7
  94.2 2.2 collective-permute-done.6
  96.3 2.2 collective-permute-done.7
  98.5 5.5 multiply_reduce_fusion.45
  105.2 118.7 %all-gather = f32[640,9,9]{2,1,0:T(8,128)} all-gather(f32[40,9,9]{2,1,0:T(8,128)} %copy.15), channel_id=2, replica_groups=mesh['tile'=16,'lev'=2] {'tile'}, dimensions={0}, use_global_device_ids=true | all-gather | bytes 220320 | tf_op jit(solution)/shard_map/all_gather | solution.py:98
  223.9 3.7 reduce_sum.568
  233.0 13.7 %multiply_add_fusion.2 = f32[40,16,1024]{2,0,1:T(8,128)S(1)} fusion(f32[40,16,1024]{2,0,1:T(8,128)} %copy-done.6, f32[40,16,1024]{2,0,1:T(8,128)} %get-tuple-element.109, f32[40]{0:T(128)S(1)} %get-tuple-element.162, f32[40]{0:T(128)S(1)} %get-tuple-element.163, f32[40]{0:T(128)S(1)} %get-tuple-element.164, f32[40]{0:T(128)S(1)} %get-tuple-element.165, ...), kind=kLoop, calls=%fused_computation.137 | loop fusion | flops 19005440 | bytes 13764160 | tf_op jit(solution)/shard_map/add | solution.py:49
  248.0 5.4 collective-permute-start.9
  253.4 5.8 multiply_add_fusion.1
  262.0 5.9 %collective-permute-start.11 = (f32[40,1,1024]{2,0,1:T(8,128)S(1)}, f32[40,1,1024]{2,0,1:T(8,128)S(1)}, u32[]{:S(2)}, u32[]{:S(2)}) collective-permute-start(f32[40,1,1024]{2,0,1:T(8,128)S(1)} %get-tuple-element.117), channel_id=1, source_target_pairs={{0,2},{2,4},{4,6},{6,8},{8,10},{10,12},{12,14},{14,16},{16,18},{18... | collective-permute-start | bytes 491528 | tf_op jit(solution)/shard_map/ppermute | solution.py:17
  269.3 5.4 collective-permute-start.17
  275.9 1.4 fusion.17
  278.6 5.0 collective-permute-start.13
  285.0 3.2 collective-permute-done.13
  288.2 3.3 fusion.20
  292.9 5.0 collective-permute-start.19
  299.2 6.1 %collective-permute-start.15 = (f32[40,1,1024]{2,0,1:T(8,128)S(1)}, f32[40,1,1024]{2,0,1:T(8,128)}, u32[]{:S(2)}, u32[]{:S(2)}) collective-permute-start(f32[40,1,1024]{2,0,1:T(8,128)S(1)} %get-tuple-element.113), channel_id=1, source_target_pairs={{0,2},{2,4},{4,6},{6,8},{8,10},{10,12},{12,14},{14,16},{16,18},{18... | collective-permute-start | bytes 491528 | tf_op jit(solution)/shard_map/ppermute | solution.py:17
  307.4 1.5 copy-done.20
  310.2 5.7 collective-permute-start.21
  318.0 24.4 %multiply_reduce_fusion = (f32[40]{0:T(128)}, f32[40]{0:T(128)}, f32[40]{0:T(128)}, f32[40]{0:T(128)}, f32[40]{0:T(128)}, /*index=5*/f32[40]{0:T(128)}, f32[40]{...) fusion(f32[40,16,1024]{2,0,1:T(8,128)} %copy-done.20, ...), kind=kLoop, calls=%fused_computation.91 | loop fusion | flops 70777080 | bytes 21961920 | tf_op jit(solution)/shard_map/reduce_sum | solution.py:58
  347.8 2.5 stack.449
  350.3 2.4 stack.442
  352.8 2.5 stack.434
  355.3 1.8 stack.425
  357.1 1.9 stack.415
  363.4 126.9 %all-gather.1 = f32[640,9,9]{2,1,0:T(8,128)} all-gather(f32[40,9,9]{2,1,0:T(8,128)} %copy.23), channel_id=3, replica_groups=mesh['tile'=16,'lev'=2] {'tile'}, dimensions={0}, use_global_device_ids=true | all-gather | bytes 220320 | tf_op jit(solution)/shard_map/all_gather | solution.py:98
  490.3 3.7 reduce_sum.739
  532.1 19.1 %multiply_add_fusion = f32[40,16,1024]{2,0,1:T(8,128)} fusion(f32[40,16,1024]{2,0,1:T(8,128)} %get-tuple-element.108, f32[40,16,1024]{2,0,1:T(8,128)} %copy-done.15, f32[40,16,1024]{2,0,1:T(8,128)} %copy-done.11, f32[40,16,1024]{2,0,1:T(8,128)} %get-tuple-element.107, f32[40,16,1024]{2,0,1:T(8,128)} %copy-done.16, f32[40,16,1024]{2,0,1:T(8,128)} %copy-done.13, ...), kind=kLoop, calls=%fused_computation.89 | loop fusion | flops 19005440 | bytes 21628480 | tf_op jit(solution)/shard_map/add | solution.py:49
  551.3 4.9 copy.26
  556.4 12.6 %add_add_fusion = f32[40,16,1024]{2,0,1:T(8,128)S(1)} fusion(f32[40,16,1024]{2,0,1:T(8,128)} %get-tuple-element.108, f32[40,16,1024]{2,0,1:T(8,128)} %copy-done.15, f32[40,16,1024]{2,0,1:T(8,128)S(1)} %copy-done.12, f32[40,16,1024]{2,0,1:T(8,128)} %get-tuple-element.107, f32[40,16,1024]{2,0,1:T(8,128)} %copy-done.16, f32[40,16,1024]{2,0,1:T(8,128)S(1)} %copy-done.14, ...), kind=kLoop, calls=%fused_computation.90 | loop fusion | flops 38666240 | bytes 32771040 | tf_op jit(solution)/shard_map/add | solution.py:111
  569.0 3.0 copy.25
  (305 shorter events, 79.9 us)
Async XLA Ops:
  7.2 25.7 %reduce-scatter.2.cloned.1.call-start = ((), (), s32[]{:S(2)}) async-start(), calls=%async_computation.1 | async-start | bytes 7864320 | tf_op jit(solution)/shard_map/reduce_scatter | solution.py:73
  34.9 14.3 %copy-start.3 = (f32[5,16,8,1024]{3,2,0,1:T(8,128)}, f32[5,16,8,1024]{3,2,0,1:T(8,128)S(1)}, u32[]{:S(2)}) copy-start(f32[5,16,8,1024]{3,2,0,1:T(8,128)S(1)} %copy.257) | copy-start | bytes 7864324
  35.0 8.3 %collective-permute-start = (f32[40,1,1024]{2,0,1:T(8,128)S(1)}, f32[40,1,1024]{2,0,1:T(8,128)S(1)}, u32[]{:S(2)}, u32[]{:S(2)}) collective-permute-start(f32[40,1,1024]{2,0,1:T(8,128)S(1)} %get-tuple-element.130), channel_id=1, source_target_pairs={{2,0},{4,2},{6,4},{8,6},{10,8},{12,10},{14,12},{16,14},{18,16},{20... | collective-permute-start | bytes 491528 | tf_op jit(solution)/shard_map/ppermute | solution.py:20
  36.3 11.5 %collective-permute-start.1 = (f32[40,1,1024]{2,0,1:T(8,128)S(1)}, f32[40,1,1024]{2,0,1:T(8,128)S(1)}, u32[]{:S(2)}, u32[]{:S(2)}) collective-permute-start(f32[40,1,1024]{2,0,1:T(8,128)S(1)} %get-tuple-element.131), channel_id=1, source_target_pairs={{0,2},{2,4},{4,6},{6,8},{8,10},{10,12},{12,14},{14,16},{16,18},{18... | collective-permute-start | bytes 491528 | tf_op jit(solution)/shard_map/ppermute | solution.py:17
  40.9 192.1 %copy-start.35 = (f32[40]{0:T(128)}, f32[40]{0:T(128)S(1)}, u32[]{:S(2)}) copy-start(f32[40]{0:T(128)S(1)} %add_divide_fusion) | copy-start | bytes 484
  50.8 9.0 %collective-permute-start.2 = (f32[40,1,1024]{2,0,1:T(8,128)}, f32[40,1,1024]{2,0,1:T(8,128)S(1)}, u32[]{:S(2)}, u32[]{:S(2)}) collective-permute-start(f32[40,1,1024]{2,0,1:T(8,128)} %get-tuple-element.128), channel_id=1, source_target_pairs={{2,0},{4,2},{6,4},{8,6},{10,8},{12,10},{14,12},{16,14},{18,16},{20... | collective-permute-start | bytes 491528 | tf_op jit(solution)/shard_map/ppermute | solution.py:20
  52.1 9.7 %collective-permute-start.3 = (f32[40,1,1024]{2,0,1:T(8,128)S(1)}, f32[40,1,1024]{2,0,1:T(8,128)S(1)}, u32[]{:S(2)}, u32[]{:S(2)}) collective-permute-start(f32[40,1,1024]{2,0,1:T(8,128)S(1)} %get-tuple-element.129), channel_id=1, source_target_pairs={{0,2},{2,4},{4,6},{6,8},{8,10},{10,12},{12,14},{14,16},{16,18},{18... | collective-permute-start | bytes 491528 | tf_op jit(solution)/shard_map/ppermute | solution.py:17
  59.6 170.9 %copy-start.39 = (f32[9]{0:T(128)}, f32[9]{0:T(128)S(1)}, u32[]{:S(2)}) copy-start(f32[9]{0:T(128)S(1)} %scatter.16) | copy-start | bytes 112
  59.6 14.9 %copy-start.30 = (f32[9,9]{1,0:T(8,128)S(1)}, f32[9,9]{1,0:T(8,128)}, u32[]{:S(2)}) copy-start(f32[9,9]{1,0:T(8,128)} %constant.100.clone) | copy-start | bytes 976
  68.2 9.0 %collective-permute-start.4 = (f32[40,1,1024]{2,0,1:T(8,128)}, f32[40,1,1024]{2,0,1:T(8,128)S(1)}, u32[]{:S(2)}, u32[]{:S(2)}) collective-permute-start(f32[40,1,1024]{2,0,1:T(8,128)} %get-tuple-element.126), channel_id=1, source_target_pairs={{2,0},{4,2},{6,4},{8,6},{10,8},{12,10},{14,12},{16,14},{18,16},{20... | collective-permute-start | bytes 491528 | tf_op jit(solution)/shard_map/ppermute | solution.py:20
  69.5 12.2 %collective-permute-start.5 = (f32[40,1,1024]{2,0,1:T(8,128)}, f32[40,1,1024]{2,0,1:T(8,128)S(1)}, u32[]{:S(2)}, u32[]{:S(2)}) collective-permute-start(f32[40,1,1024]{2,0,1:T(8,128)} %get-tuple-element.127), channel_id=1, source_target_pairs={{0,2},{2,4},{4,6},{6,8},{8,10},{10,12},{12,14},{14,16},{16,18},{18... | collective-permute-start | bytes 491528 | tf_op jit(solution)/shard_map/ppermute | solution.py:17
  74.7 157.5 %copy-start.24 = (f32[40,9]{0,1:T(8,128)}, f32[40,9]{0,1:T(8,128)S(1)}, u32[]{:S(2)}) copy-start(f32[40,9]{0,1:T(8,128)S(1)} %convolution_subtract_fusion.6) | copy-start | bytes 4324
  74.8 154.2 %copy-start.33 = (f32[40,9]{1,0:T(8,128)}, f32[40,9]{1,0:T(8,128)S(1)}, u32[]{:S(2)}) copy-start(f32[40,9]{1,0:T(8,128)S(1)} %copy.44) | copy-start | bytes 4324
  74.8 19.1 %copy-start.2 = (f32[40,16384]{1,0:T(8,128)S(1)}, f32[40,16384]{1,0:T(8,128)}, u32[]{:S(2)}) copy-start(f32[40,16384]{1,0:T(8,128)} %reduce-scatter.2.cloned.1.call-done) | copy-start | bytes 7864324
  81.7 171.7 %copy-start.21 = (f32[40,1,1024]{2,0,1:T(8,128)}, f32[40,1,1024]{2,0,1:T(8,128)S(1)}, u32[]{:S(2)}) copy-start(f32[40,1,1024]{2,0,1:T(8,128)S(1)} %collective-permute-done.5) | copy-start | bytes 491524
  87.3 11.2 %copy-start.19 = (f32[40,16,1024]{2,0,1:T(8,128)S(1)}, f32[40,16,1024]{2,0,1:T(8,128)}, u32[]{:S(2)}) copy-start(f32[40,16,1024]{2,0,1:T(8,128)} %copy-done.18) | copy-start | bytes 7864324
  87.3 11.2 %copy-start.27 = (f32[40,1,1024]{2,0,1:T(8,128)S(1)}, f32[40,1,1024]{2,0,1:T(8,128)}, u32[]{:S(2)}) copy-start(f32[40,1,1024]{2,0,1:T(8,128)} %copy-done.26) | copy-start | bytes 491524
  87.3 11.2 %copy-start.29 = (f32[40,1,1024]{2,0,1:T(8,128)S(1)}, f32[40,1,1024]{2,0,1:T(8,128)}, u32[]{:S(2)}) copy-start(f32[40,1,1024]{2,0,1:T(8,128)} %copy-done.28) | copy-start | bytes 491524
  87.4 8.9 %collective-permute-start.6 = (f32[40,1,1024]{2,0,1:T(8,128)S(1)}, f32[40,1,1024]{2,0,1:T(8,128)S(1)}, u32[]{:S(2)}, u32[]{:S(2)}) collective-permute-start(f32[40,1,1024]{2,0,1:T(8,128)S(1)} %get-tuple-element.124), channel_id=1, source_target_pairs={{2,0},{4,2},{6,4},{8,6},{10,8},{12,10},{14,12},{16,14},{18,16},{20... | collective-permute-start | bytes 491528 | tf_op jit(solution)/shard_map/ppermute | solution.py:20
  88.9 9.6 %collective-permute-start.7 = (f32[40,1,1024]{2,0,1:T(8,128)S(1)}, f32[40,1,1024]{2,0,1:T(8,128)S(1)}, u32[]{:S(2)}, u32[]{:S(2)}) collective-permute-start(f32[40,1,1024]{2,0,1:T(8,128)S(1)} %get-tuple-element.125), channel_id=1, source_target_pairs={{0,2},{2,4},{4,6},{6,8},{8,10},{10,12},{12,14},{14,16},{16,18},{18... | collective-permute-start | bytes 491528 | tf_op jit(solution)/shard_map/ppermute | solution.py:17
  233.0 20.4 %copy-start.4 = (f32[5,16,8,1024]{3,2,0,1:T(8,128)S(1)}, f32[5,16,8,1024]{3,2,0,1:T(8,128)}, u32[]{:S(2)}) copy-start(f32[5,16,8,1024]{3,2,0,1:T(8,128)} %copy-done.3) | copy-start | bytes 7864324
  233.0 20.4 %copy-start.7 = (f32[40,16,1024]{2,0,1:T(8,128)S(1)}, f32[40,16,1024]{2,0,1:T(8,128)}, u32[]{:S(2)}) copy-start(f32[40,16,1024]{2,0,1:T(8,128)} %copy-done.6) | copy-start | bytes 7864324
  233.0 20.4 %copy-start.17 = (f32[40,16,1024]{2,0,1:T(8,128)S(1)}, f32[40,16,1024]{2,0,1:T(8,128)}, u32[]{:S(2)}) copy-start(f32[40,16,1024]{2,0,1:T(8,128)} %get-tuple-element.109) | copy-start | bytes 7864324
  246.7 71.3 %copy-start.9 = (f32[40,16,1024]{2,0,1:T(8,128)}, f32[40,16,1024]{2,0,1:T(8,128)S(1)}, u32[]{:S(2)}) copy-start(f32[40,16,1024]{2,0,1:T(8,128)S(1)} %multiply_add_fusion.2) | copy-start | bytes 7864324
  246.7 12.5 %collective-permute-start.8 = (f32[40,1,1024]{2,0,1:T(8,128)S(1)}, f32[40,1,1024]{2,0,1:T(8,128)S(1)}, u32[]{:S(2)}, u32[]{:S(2)}) collective-permute-start(f32[40,1,1024]{2,0,1:T(8,128)S(1)} %get-tuple-element.118), channel_id=1, source_target_pairs={{2,0},{4,2},{6,4},{8,6},{10,8},{12,10},{14,12},{16,14},{18,16},{20... | collective-permute-start | bytes 491528 | tf_op jit(solution)/shard_map/ppermute | solution.py:20
  248.0 11.2 %collective-permute-start.9 = (f32[40,1,1024]{2,0,1:T(8,128)S(1)}, f32[40,1,1024]{2,0,1:T(8,128)S(1)}, u32[]{:S(2)}, u32[]{:S(2)}) collective-permute-start(f32[40,1,1024]{2,0,1:T(8,128)S(1)} %get-tuple-element.119), channel_id=1, source_target_pairs={{0,2},{2,4},{4,6},{6,8},{8,10},{10,12},{12,14},{14,16},{16,18},{18... | collective-permute-start | bytes 491528 | tf_op jit(solution)/shard_map/ppermute | solution.py:17
  259.2 58.8 %copy-start.11 = (f32[40,16,1024]{2,0,1:T(8,128)}, f32[40,16,1024]{2,0,1:T(8,128)S(1)}, u32[]{:S(2)}) copy-start(f32[40,16,1024]{2,0,1:T(8,128)S(1)} %multiply_add_fusion.1) | copy-start | bytes 7864324
  260.7 57.3 %copy-start.13 = (f32[40,16,1024]{2,0,1:T(8,128)}, f32[40,16,1024]{2,0,1:T(8,128)S(1)}, u32[]{:S(2)}) copy-start(f32[40,16,1024]{2,0,1:T(8,128)S(1)} %fusion.14) | copy-start | bytes 7864324
  260.7 14.0 %collective-permute-start.10 = (f32[40,1,1024]{2,0,1:T(8,128)S(1)}, f32[40,1,1024]{2,0,1:T(8,128)S(1)}, u32[]{:S(2)}, u32[]{:S(2)}) collective-permute-start(f32[40,1,1024]{2,0,1:T(8,128)S(1)} %get-tuple-element.116), channel_id=1, source_target_pairs={{2,0},{4,2},{6,4},{8,6},{10,8},{12,10},{14,12},{16,14},{18,16},{20... | collective-permute-start | bytes 491528 | tf_op jit(solution)/shard_map/ppermute | solution.py:20
  262.0 13.8 %collective-permute-start.11 = (f32[40,1,1024]{2,0,1:T(8,128)S(1)}, f32[40,1,1024]{2,0,1:T(8,128)S(1)}, u32[]{:S(2)}, u32[]{:S(2)}) collective-permute-start(f32[40,1,1024]{2,0,1:T(8,128)S(1)} %get-tuple-element.117), channel_id=1, source_target_pairs={{0,2},{2,4},{4,6},{6,8},{8,10},{10,12},{12,14},{14,16},{16,18},{18... | collective-permute-start | bytes 491528 | tf_op jit(solution)/shard_map/ppermute | solution.py:17
  268.0 15.7 %collective-permute-start.16 = (f32[40,1,1024]{2,0,1:T(8,128)S(1)}, f32[40,1,1024]{2,0,1:T(8,128)S(1)}, u32[]{:S(2)}, u32[]{:S(2)}) collective-permute-start(f32[40,1,1024]{2,0,1:T(8,128)S(1)} %get-tuple-element.122), channel_id=1, source_target_pairs={{2,0},{4,2},{6,4},{8,6},{10,8},{12,10},{14,12},{16,14},{18,16},{20... | collective-permute-start | bytes 491528 | tf_op jit(solution)/shard_map/ppermute | solution.py:20
  269.3 14.4 %collective-permute-start.17 = (f32[40,1,1024]{2,0,1:T(8,128)S(1)}, f32[40,1,1024]{2,0,1:T(8,128)S(1)}, u32[]{:S(2)}, u32[]{:S(2)}) collective-permute-start(f32[40,1,1024]{2,0,1:T(8,128)S(1)} %get-tuple-element.123), channel_id=1, source_target_pairs={{0,2},{2,4},{4,6},{6,8},{8,10},{10,12},{12,14},{14,16},{16,18},{18... | collective-permute-start | bytes 491528 | tf_op jit(solution)/shard_map/ppermute | solution.py:17
  277.3 7.7 %collective-permute-start.12 = (f32[40,1,1024]{2,0,1:T(8,128)S(1)}, f32[40,1,1024]{2,0,1:T(8,128)S(1)}, u32[]{:S(2)}, u32[]{:S(2)}) collective-permute-start(f32[40,1,1024]{2,0,1:T(8,128)S(1)} %get-tuple-element.114), channel_id=1, source_target_pairs={{2,0},{4,2},{6,4},{8,6},{10,8},{12,10},{14,12},{16,14},{18,16},{20... | collective-permute-start | bytes 491528 | tf_op jit(solution)/shard_map/ppermute | solution.py:20
  278.6 9.6 %collective-permute-start.13 = (f32[40,1,1024]{2,0,1:T(8,128)S(1)}, f32[40,1,1024]{2,0,1:T(8,128)S(1)}, u32[]{:S(2)}, u32[]{:S(2)}) collective-permute-start(f32[40,1,1024]{2,0,1:T(8,128)S(1)} %get-tuple-element.115), channel_id=1, source_target_pairs={{0,2},{2,4},{4,6},{6,8},{8,10},{10,12},{12,14},{14,16},{16,18},{18... | collective-permute-start | bytes 491528 | tf_op jit(solution)/shard_map/ppermute | solution.py:17
  291.6 15.8 %copy-start.15 = (f32[40,16,1024]{2,0,1:T(8,128)}, f32[40,16,1024]{2,0,1:T(8,128)S(1)}, u32[]{:S(2)}) copy-start(f32[40,16,1024]{2,0,1:T(8,128)S(1)} %get-tuple-element.182) | copy-start | bytes 7864324
  291.6 15.8 %copy-start.16 = (f32[40,16,1024]{2,0,1:T(8,128)}, f32[40,16,1024]{2,0,1:T(8,128)S(1)}, u32[]{:S(2)}) copy-start(f32[40,16,1024]{2,0,1:T(8,128)S(1)} %get-tuple-element.181) | copy-start | bytes 7864324
  291.6 13.7 %collective-permute-start.18 = (f32[40,1,1024]{2,0,1:T(8,128)S(1)}, f32[40,1,1024]{2,0,1:T(8,128)S(1)}, u32[]{:S(2)}, u32[]{:S(2)}) collective-permute-start(f32[40,1,1024]{2,0,1:T(8,128)S(1)} %get-tuple-element.120), channel_id=1, source_target_pairs={{2,0},{4,2},{6,4},{8,6},{10,8},{12,10},{14,12},{16,14},{18,16},{20... | collective-permute-start | bytes 491528 | tf_op jit(solution)/shard_map/ppermute | solution.py:20
  292.9 13.0 %collective-permute-start.19 = (f32[40,1,1024]{2,0,1:T(8,128)S(1)}, f32[40,1,1024]{2,0,1:T(8,128)S(1)}, u32[]{:S(2)}, u32[]{:S(2)}) collective-permute-start(f32[40,1,1024]{2,0,1:T(8,128)S(1)} %get-tuple-element.121), channel_id=1, source_target_pairs={{0,2},{2,4},{4,6},{6,8},{8,10},{10,12},{12,14},{14,16},{16,18},{18... | collective-permute-start | bytes 491528 | tf_op jit(solution)/shard_map/ppermute | solution.py:17
  297.9 18.5 %collective-permute-start.14 = (f32[40,1,1024]{2,0,1:T(8,128)S(1)}, f32[40,1,1024]{2,0,1:T(8,128)}, u32[]{:S(2)}, u32[]{:S(2)}) collective-permute-start(f32[40,1,1024]{2,0,1:T(8,128)S(1)} %get-tuple-element.112), channel_id=1, source_target_pairs={{2,0},{4,2},{6,4},{8,6},{10,8},{12,10},{14,12},{16,14},{18,16},{20... | collective-permute-start | bytes 491528 | tf_op jit(solution)/shard_map/ppermute | solution.py:20
  299.2 17.2 %collective-permute-start.15 = (f32[40,1,1024]{2,0,1:T(8,128)S(1)}, f32[40,1,1024]{2,0,1:T(8,128)}, u32[]{:S(2)}, u32[]{:S(2)}) collective-permute-start(f32[40,1,1024]{2,0,1:T(8,128)S(1)} %get-tuple-element.113), channel_id=1, source_target_pairs={{0,2},{2,4},{4,6},{6,8},{8,10},{10,12},{12,14},{14,16},{16,18},{18... | collective-permute-start | bytes 491528 | tf_op jit(solution)/shard_map/ppermute | solution.py:17
  308.9 7.8 %collective-permute-start.20 = (f32[40,1,1024]{2,0,1:T(8,128)S(1)}, f32[40,1,1024]{2,0,1:T(8,128)}, u32[]{:S(2)}, u32[]{:S(2)}) collective-permute-start(f32[40,1,1024]{2,0,1:T(8,128)S(1)} %get-tuple-element.110), channel_id=1, source_target_pairs={{2,0},{4,2},{6,4},{8,6},{10,8},{12,10},{14,12},{16,14},{18,16},{20... | collective-permute-start | bytes 491528 | tf_op jit(solution)/shard_map/ppermute | solution.py:20
  310.2 7.8 %collective-permute-start.21 = (f32[40,1,1024]{2,0,1:T(8,128)S(1)}, f32[40,1,1024]{2,0,1:T(8,128)}, u32[]{:S(2)}, u32[]{:S(2)}) collective-permute-start(f32[40,1,1024]{2,0,1:T(8,128)S(1)} %get-tuple-element.111), channel_id=1, source_target_pairs={{0,2},{2,4},{4,6},{6,8},{8,10},{10,12},{12,14},{14,16},{16,18},{18... | collective-permute-start | bytes 491528 | tf_op jit(solution)/shard_map/ppermute | solution.py:17
  490.3 10.6 %copy-start.25 = (f32[40,9]{0,1:T(8,128)S(1)}, f32[40,9]{0,1:T(8,128)}, u32[]{:S(2)}) copy-start(f32[40,9]{0,1:T(8,128)} %copy-done.24) | copy-start | bytes 4324
  490.3 16.7 %copy-start.31 = (f32[9,9]{1,0:T(8,128)S(1)}, f32[9,9]{1,0:T(8,128)}, u32[]{:S(2)}) copy-start(f32[9,9]{1,0:T(8,128)} %constant.100.clone) | copy-start | bytes 976
  532.1 24.1 %copy-start.10 = (f32[40,16,1024]{2,0,1:T(8,128)S(1)}, f32[40,16,1024]{2,0,1:T(8,128)}, u32[]{:S(2)}) copy-start(f32[40,16,1024]{2,0,1:T(8,128)} %copy-done.9) | copy-start | bytes 7864324
  532.1 24.1 %copy-start.12 = (f32[40,16,1024]{2,0,1:T(8,128)S(1)}, f32[40,16,1024]{2,0,1:T(8,128)}, u32[]{:S(2)}) copy-start(f32[40,16,1024]{2,0,1:T(8,128)} %copy-done.11) | copy-start | bytes 7864324
  532.1 24.1 %copy-start.14 = (f32[40,16,1024]{2,0,1:T(8,128)S(1)}, f32[40,16,1024]{2,0,1:T(8,128)}, u32[]{:S(2)}) copy-start(f32[40,16,1024]{2,0,1:T(8,128)} %copy-done.13) | copy-start | bytes 7864324
  556.4 15.6 %copy-start.1 = (bf16[80,136]{0,1:T(8,128)(2,1)S(1)}, bf16[80,136]{0,1:T(8,128)(2,1)}, u32[]{:S(2)}) copy-start(bf16[80,136]{0,1:T(8,128)(2,1)} %param.13) | copy-start | bytes 65284
  (38 other events, 137.8 us)
Sparse Core Ops, SparseCore 0:
  17.1 15.7 reduce-scatter.1
